TPU v7x, 32 devices: a whole 2x2x4 slice. The times are simulated.
32 devices in a mesh: seq: 8 (over z, core), tp: 4 (over y, x).
Axes of the slice: x: 2, y: 2, z: 4, core: 2. Of those that a mesh axis runs over, the one named last changes fastest.
Arguments:
- hidden: bfloat16 [4096, 2048], P(('seq', 'tp')), may hold values from -5 to 5
- w_qkv: bfloat16 [2048, 3, 2048], P(None, None, 'tp'), may hold values from -0.125 to 0.125
- w_gate: bfloat16 [2048, 2048], P(None, 'tp'), may hold values from -0.125 to 0.125
- w_decay_beta: bfloat16 [2048, 2, 16], P(None, None, 'tp'), may hold values from -0.7 to 0.7
- conv_weight: bfloat16 [4, 3, 2048], P(None, None, 'tp'), may hold values from -2 to 2
- decay_rate: float32 [16], P('tp'), may hold values from 2e-05 to 0.05
- dt_bias: float32 [16], P('tp'), may hold values from -1 to 1
- norm_gain: float32 [128], replicated, may hold values from 0.1 to 1.9
Outputs:
- core: bfloat16 [4096, 2048], P('seq', 'tp')
All inputs are finite; a program needn't handle non-finite values.
Results may differ from a plain program's by a relative error of at most 0.01.
Values may be sent and summed in bfloat16 or wider, within the bound.
A program may use at most 64 MiB of HBM per device.

v0:
```python
import functools
import math

import jax
import jax.numpy as jnp
from jax import lax
from jax.experimental import pallas as pl
from jax.experimental.pallas import tpu as pltpu
from jax.sharding import PartitionSpec as P

MESH = pl.DeviceIdType.MESH
CHUNK = 128
RIM = 16
NT = (((1,), (1,)), ((), ()))
TN = (((0,), (0,)), ((), ()))


def low(value):
    return value.astype(jnp.bfloat16)


def dot(left, right, dims=(((1,), (0,)), ((), ()))):
    return lax.dot_general(low(left), low(right), dims, preferred_element_type=jnp.float32)


def peer_of(me, step, count):
    if count & (count - 1):
        return lax.rem(me + step, count)
    bit = 1
    while bit < count:
        if step & bit:
            me = me + bit - 2 * bit * lax.rem(me // bit, 2)
        bit *= 2
    return me


def silu(value):
    return value / (1.0 + jnp.exp(-value))


def unit_rows(matrix):
    return matrix * lax.rsqrt(jnp.sum(matrix * matrix, axis=-1, keepdims=True) + 1e-06)


def kernel(
    n_seq, n_tp, rate_ref, bias_ref, hidden, w_qkv, w_gate, wdb_ref, conv_ref, gain_ref, out_ref,
    tokens, rim, weights, proj, state, outs, deltas, st_in, st_out,
    tok_send, tok_recv, w_sem, rim_send, rim_recv, st_send, st_recv,
):
    seq, me = lax.axis_index("seq"), lax.axis_index("tp")
    rows = hidden.shape[0]
    total = tokens.shape[0]
    heads = rate_ref.shape[0]
    head_dim = gain_ref.shape[1]
    taps = conv_ref.shape[1]
    last_tp, last_seq = n_tp - 1, n_seq - 1

    own = pltpu.make_async_copy(hidden, tokens.at[pl.ds(me * rows, rows)], tok_recv.at[0])
    own.start()
    loads = [pltpu.make_async_copy(w_qkv.at[b], weights.at[b], w_sem.at[b]) for b in range(3)]
    loads.append(pltpu.make_async_copy(w_gate, weights.at[3], w_sem.at[3]))
    for load in loads:
        load.start()

    barrier = pltpu.get_barrier_semaphore()

    def greet(where):
        pl.semaphore_signal(barrier, inc=1, device_id=where, device_id_type=MESH)

    for step in range(1, n_tp):
        greet({"tp": peer_of(me, step, n_tp)})

    @pl.when(seq > 0)
    def _():
        greet({"seq": seq - 1})

        @pl.when(me < last_tp)
        def _():
            greet({"seq": seq - 1, "tp": last_tp})

    @pl.when(seq < last_seq)
    def _():
        greet({"seq": seq + 1})

    before = (seq + last_seq) // n_seq
    after = (2 * last_seq - seq) // n_seq
    tail_owner = (me + 1) // n_tp
    pl.semaphore_wait(barrier, last_tp + before + after + after * tail_owner * last_tp)

    def token_copy(step):
        peer = peer_of(me, step, n_tp)
        return pltpu.make_async_remote_copy(
            src_ref=hidden,
            dst_ref=tokens.at[pl.ds(me * rows, rows)],
            send_sem=tok_send.at[step],
            recv_sem=tok_recv.at[step],
            device_id={"tp": peer},
            device_id_type=MESH,
        )

    def rim_copy(target):
        return pltpu.make_async_remote_copy(
            src_ref=hidden.at[pl.ds(rows - RIM, RIM)],
            dst_ref=rim,
            send_sem=rim_send.at[target],
            recv_sem=rim_recv,
            device_id={"seq": seq + 1, "tp": target},
            device_id_type=MESH,
        )

    for step in range(1, n_tp):
        token_copy(step).start()

    @pl.when(jnp.logical_and(seq < last_seq, me == last_tp))
    def _():
        for target in range(n_tp):
            rim_copy(target).start()

    @pl.when(seq == 0)
    def _():
        rim[...] = jnp.zeros_like(rim)
        st_in[...] = jnp.zeros_like(st_in)

    for load in loads:
        load.wait()

    def project(block, at):
        def one(b, carry):
            full = jnp.dot(block, weights[b], preferred_element_type=jnp.float32)
            rounded = full.astype(jnp.bfloat16).astype(jnp.float32)
            proj[b, pl.ds(pl.multiple_of(at, 16), block.shape[0]), :] = jnp.where(b < 3, rounded, full)
            return carry

        lax.fori_loop(0, 4, one, 0)

    for step in range(n_tp):
        if step == 0:
            own.wait()
        else:
            token_copy(step).wait_recv()
        if n_tp & (n_tp - 1):
            slot = lax.rem(me - step + n_tp, n_tp)
        else:
            slot = peer_of(me, step, n_tp)
        at = pl.multiple_of(slot * rows, 16)
        project(tokens[pl.ds(at, rows), :], RIM + at)

    @pl.when(seq > 0)
    def _():
        pltpu.make_async_copy(hidden.at[pl.ds(0, RIM)], rim, rim_recv).wait()

    project(rim[...], 0)

    down = lax.broadcasted_iota(jnp.int32, (CHUNK, CHUNK), 0)
    across = lax.broadcasted_iota(jnp.int32, (CHUNK, CHUNK), 1)
    eye = (down == across).astype(jnp.float32)
    wide = lax.broadcasted_iota(jnp.int32, (head_dim, 2 * head_dim), 0) + head_dim
    start = (wide == lax.broadcasted_iota(jnp.int32, (head_dim, 2 * head_dim), 1)).astype(jnp.float32)
    for h in range(heads):
        state[h] = start

    def chunk(c, carry):
        r0 = pl.multiple_of(c * CHUNK, CHUNK)
        scalars = lax.dot_general(
            wdb_ref[...], tokens[pl.ds(r0, CHUNK), :], NT, preferred_element_type=jnp.float32
        )
        per_head = []
        for h in range(heads):
            cols = slice(h * head_dim, (h + 1) * head_dim)
            branch = []
            for b in range(3):
                window = proj[b, pl.ds(r0 + 8, CHUNK + 8), cols]
                conv = jnp.zeros((CHUNK, head_dim), jnp.float32)
                for i in range(taps):
                    offset = 9 - taps + i
                    tap = conv_ref[b, i : i + 1, cols].astype(jnp.float32)
                    conv = conv + window[offset : offset + CHUNK] * tap
                branch.append(silu(conv).astype(jnp.bfloat16).astype(jnp.float32))
            q = unit_rows(branch[0]) * (1.0 / math.sqrt(head_dim))
            k = unit_rows(branch[1])
            v = branch[2]
            u = scalars[h : h + 1, :] + bias_ref[h]
            log_row = -rate_ref[h] * (jnp.maximum(u, 0.0) + jnp.log1p(jnp.exp(-jnp.abs(u))))
            rate_row = 1.0 / (1.0 + jnp.exp(-scalars[heads + h : heads + h + 1, :]))
            cum_col = jnp.sum(jnp.where(across <= down, log_row, 0.0), axis=1, keepdims=True)
            cum_row = jnp.sum(jnp.where(across == down, cum_col, 0.0), axis=0, keepdims=True)
            rate_col = jnp.sum(jnp.where(across == down, rate_row, 0.0), axis=1, keepdims=True)
            end = cum_col[CHUNK - 1 : CHUNK, :]
            gap = jnp.exp(jnp.where(across <= down, cum_col - cum_row, 0.0))
            weight = jnp.where(across <= down, gap, 0.0) * rate_row
            mixing = jnp.where(across < down, weight * dot(k, k, NT), 0.0)
            attend = weight * dot(q, k, NT)
            run = jnp.exp(cum_col)
            tail = rate_col * jnp.exp(end - cum_col)
            per_head.append((q * run, k * run, v, k * tail, mixing, attend, jnp.exp(end)))
        inverse = [eye] * heads
        size = 1
        while size < CHUNK:
            half = (down // size) % 2 == 1
            lower = jnp.logical_and(half, across // size == down // size - 1)
            for h in range(heads):
                part = jnp.where(lower, per_head[h][4], 0.0)
                if size == 1:
                    inverse[h] = eye - part
                else:
                    inverse[h] = inverse[h] - dot(dot(inverse[h], part), inverse[h])
            size *= 2
        for h in range(heads):
            q_run, k_run, v, k_tail, _, attend, fade = per_head[h]
            solved = dot(inverse[h], jnp.concatenate([v, k_run], axis=1))
            held = state[h]
            fresh = solved[:, :head_dim]
            fresh = jnp.concatenate([fresh, jnp.zeros_like(fresh)], axis=1)
            fresh = fresh - dot(solved[:, head_dim:], held)
            read = dot(q_run, held) + dot(attend, fresh)
            state[h] = fade * held + dot(k_tail, fresh, TN)
            outs[h, pl.ds(r0, CHUNK), :] = read[:, :head_dim]
            deltas[h, pl.ds(r0, CHUNK), :] = low(read[:, head_dim:])
        return carry

    lax.fori_loop(0, total // CHUNK, chunk, 0)

    def state_copy(h):
        return pltpu.make_async_remote_copy(
            src_ref=st_out.at[h],
            dst_ref=st_in.at[h],
            send_sem=st_send.at[h],
            recv_sem=st_recv.at[h],
            device_id={"seq": seq + 1},
            device_id_type=MESH,
        )

    for h in range(heads):

        @pl.when(seq > 0)
        def _():
            pltpu.make_async_copy(st_out.at[h], st_in.at[h], st_recv.at[h]).wait()

        @pl.when(seq < last_seq)
        def _():
            mine = state[h]
            st_out[h] = low(mine[:, :head_dim] + dot(mine[:, head_dim:], st_in[h]))
            state_copy(h).start()

    for h in range(heads):
        cols = slice(h * head_dim, (h + 1) * head_dim)
        read = outs[h] + dot(deltas[h], st_in[h])
        scale = lax.rsqrt(jnp.mean(read * read, axis=-1, keepdims=True) + 1e-06)
        gate = silu(proj[3, pl.ds(RIM, total), cols])
        out_ref[:, cols] = low(read * scale * gain_ref[...] * gate)

    for step in range(1, n_tp):
        token_copy(step).wait_send()

    @pl.when(jnp.logical_and(seq < last_seq, me == last_tp))
    def _():
        for target in range(n_tp):
            rim_copy(target).wait_send()

    @pl.when(seq < last_seq)
    def _():
        for h in range(heads):
            state_copy(h).wait_send()


def per_device(
    n_seq, n_tp, hidden, w_qkv, w_gate, w_decay_beta, conv_weight, decay_rate, dt_bias, norm_gain
):
    width = hidden.shape[1]
    heads = decay_rate.shape[0]
    head_dim = norm_gain.shape[0]
    columns = heads * head_dim
    rows = hidden.shape[0]
    total = rows * n_tp
    wdb = w_decay_beta.transpose(1, 2, 0).reshape(2 * heads, width)
    vmem, smem, anywhere = (
        pl.BlockSpec(memory_space=pltpu.VMEM),
        pl.BlockSpec(memory_space=pltpu.SMEM),
        pl.BlockSpec(memory_space=pl.ANY),
    )
    dma = pltpu.SemaphoreType.DMA
    return pl.pallas_call(
        functools.partial(kernel, n_seq, n_tp),
        out_shape=jax.ShapeDtypeStruct((total, columns), jnp.bfloat16),
        in_specs=[smem, smem, anywhere, anywhere, anywhere, vmem, vmem, vmem],
        out_specs=vmem,
        scratch_shapes=[
            pltpu.VMEM((total, width), jnp.bfloat16),
            pltpu.VMEM((RIM, width), jnp.bfloat16),
            pltpu.VMEM((4, width, columns), jnp.bfloat16),
            pltpu.VMEM((4, RIM + total, columns), jnp.float32),
            pltpu.VMEM((heads, head_dim, 2 * head_dim), jnp.float32),
            pltpu.VMEM((heads, total, head_dim), jnp.float32),
            pltpu.VMEM((heads, total, head_dim), jnp.bfloat16),
            pltpu.VMEM((heads, head_dim, head_dim), jnp.bfloat16),
            pltpu.VMEM((heads, head_dim, head_dim), jnp.bfloat16),
            dma((n_tp,)),
            dma((n_tp,)),
            dma((4,)),
            dma((n_tp,)),
            dma,
            dma((heads,)),
            dma((heads,)),
        ],
        compiler_params=pltpu.CompilerParams(
            collective_id=0, has_side_effects=True, vmem_limit_bytes=50 * 1024 * 1024
        ),
    )(
        decay_rate, dt_bias, hidden, w_qkv.transpose(1, 0, 2), w_gate, wdb,
        conv_weight.transpose(1, 0, 2), norm_gain.reshape(1, head_dim),
    )


def solution(mesh):
    return jax.shard_map(
        functools.partial(per_device, mesh.shape["seq"], mesh.shape["tp"]),
        mesh=mesh,
        in_specs=(
            P(("seq", "tp"), None),
            P(None, None, "tp"),
            P(None, "tp"),
            P(None, None, "tp"),
            P(None, None, "tp"),
            P("tp"),
            P("tp"),
            P(),
        ),
        out_specs=P("seq", "tp"),
        check_vma=False,
    )
```

profile of v0, /device:TPU:25, one launch (start us, length us, event | category | flops | bytes accessed | tf_op | source)
XLA Modules:
  0.0 65.0 jit_solution(4200936190397765472)
XLA Ops:
  0.0 0.8 %reshape.6.wdb_ref = bf16[8,2048]{1,0:T(8,128)(2,1)S(1)} reshape(bf16[2,4,2048]{2,1,0:T(4,128)(2,1)} %bitcast.7) | data formatting | bytes 65536 | tf_op jit(solution)/shard_map/reshape | solution.py:275
  0.8 0.0 copy-start
  0.8 1.6 %copy-done = bf16[2048,512]{1,0:T(8,128)(2,1)S(1)} copy-done((bf16[2048,512]{1,0:T(8,128)(2,1)S(1)}, bf16[2048,512]{1,0:T(8,128)(2,1)}, u32[]{:S(2)}) %copy-start) | copy-done | bytes 2097176
  2.4 0.0 copy-start.1
  2.4 1.0 %copy-done.1 = bf16[128,2048]{1,0:T(8,128)(2,1)S(1)} copy-done((bf16[128,2048]{1,0:T(8,128)(2,1)S(1)}, bf16[128,2048]{1,0:T(8,128)(2,1)}, u32[]{:S(2)}) %copy-start.1) | copy-done | bytes 524312
  3.4 0.0 copy-start.2
  3.4 0.7 %copy-done.2 = bf16[4,3,512]{2,0,1:T(4,128)(2,1)S(1)} copy-done((bf16[4,3,512]{2,0,1:T(4,128)(2,1)S(1)}, bf16[4,3,512]{2,0,1:T(4,128)(2,1)}, u32[]{:S(2)}) %copy-start.2) | copy-done | bytes 12312
  4.1 0.0 copy-start.3
  4.1 0.7 %copy-done.3 = f32[4]{0:T(128)S(1)} copy-done((f32[4]{0:T(128)S(1)}, f32[4]{0:T(128)}, u32[]{:S(2)}) %copy-start.3) | copy-done | bytes 40
  4.8 0.0 copy-start.4
  4.8 0.7 %copy-done.4 = f32[4]{0:T(128)S(1)} copy-done((f32[4]{0:T(128)S(1)}, f32[4]{0:T(128)}, u32[]{:S(2)}) %copy-start.4) | copy-done | bytes 40
  5.4 0.0 copy-start.5
  5.4 0.7 %copy-done.5 = f32[128]{0:T(128)S(1)} copy-done((f32[128]{0:T(128)S(1)}, f32[128]{0:T(128)}, u32[]{:S(2)}) %copy-start.5) | copy-done | bytes 536
  6.1 58.2 %shard_map.82 = bf16[512,512]{1,0:T(8,128)(2,1)S(1)} custom-call(f32[4]{0:T(128)S(1)} %copy-done.3, f32[4]{0:T(128)S(1)} %copy-done.4, bf16[128,2048]{1,0:T(8,128)(2,1)S(1)} %copy-done.1, bf16[3,2048,512]{2,1,0:T(8,128)(2,1)} %bitcast.6, bf16[2048,512]{1,0:T(8,128)(2,1)S(1)} %copy-done, bf16[8,2048]{1,0:T(8,128)(2,1)S(1)} %reshape.6.wdb_ref, ...), custom_call_target="tpu_custom_call" | custom-call | tf_op jit(solution)/shard_map/pallas_call | solution.py:282
  64.2 0.8 %copy.10 = bf16[512,512]{1,0:T(8,128)(2,1)} copy(bf16[512,512]{1,0:T(8,128)(2,1)S(1)} %shard_map.82) | data formatting | bytes 1048576
Async XLA Ops:
  0.8 1.6 %copy-start = (bf16[2048,512]{1,0:T(8,128)(2,1)S(1)}, bf16[2048,512]{1,0:T(8,128)(2,1)}, u32[]{:S(2)}) copy-start(bf16[2048,512]{1,0:T(8,128)(2,1)} %w_gate.1) | copy-start | bytes 6291460
  2.4 1.0 %copy-start.1 = (bf16[128,2048]{1,0:T(8,128)(2,1)S(1)}, bf16[128,2048]{1,0:T(8,128)(2,1)}, u32[]{:S(2)}) copy-start(bf16[128,2048]{1,0:T(8,128)(2,1)} %hidden.1) | copy-start | bytes 1572868
  3.4 0.7 %copy-start.2 = (bf16[4,3,512]{2,0,1:T(4,128)(2,1)S(1)}, bf16[4,3,512]{2,0,1:T(4,128)(2,1)}, u32[]{:S(2)}) copy-start(bf16[4,3,512]{2,0,1:T(4,128)(2,1)} %param.12) | copy-start | bytes 36868
  4.1 0.7 %copy-start.3 = (f32[4]{0:T(128)S(1)}, f32[4]{0:T(128)}, u32[]{:S(2)}) copy-start(f32[4]{0:T(128)} %rate_ref.1) | copy-start | bytes 52
  4.8 0.7 %copy-start.4 = (f32[4]{0:T(128)S(1)}, f32[4]{0:T(128)}, u32[]{:S(2)}) copy-start(f32[4]{0:T(128)} %bias_ref.1) | copy-start | bytes 52
  5.4 0.7 %copy-start.5 = (f32[128]{0:T(128)S(1)}, f32[128]{0:T(128)}, u32[]{:S(2)}) copy-start(f32[128]{0:T(128)} %param.15) | copy-start | bytes 1540
where the time goes:
time: 65.5 us; the launch traced here: 65 us
  Pallas kernels  58.2 us (89%)
  local copies, waits for them, and re-layouts  6.86 us (10%)
    pallas_call x1, Pallas kernels, per_device(): pl.pallas_call(functools.partial(kernel, n_seq, n_tp), out_shape=jax.Shap...  58.2 us
    unnamed x13, local copies, waits for them, and re-layouts  6.09 us

commit v1 on v0

--- a/solution.py
+++ b/solution.py
@@ -43,23 +43,29 @@
 
 
 def kernel(
-    n_seq, n_tp, rate_ref, bias_ref, hidden, w_qkv, w_gate, wdb_ref, conv_ref, gain_ref, out_ref,
+    n_seq, n_tp, rate_hbm, bias_hbm, hidden, w_qkv, w_gate, wdb_hbm, conv_hbm, gain_hbm, out_ref,
+    rate_ref, bias_ref, wdb_ref, conv_ref, gain_ref, small_sem,
     tokens, rim, weights, proj, state, outs, deltas, st_in, st_out,
     tok_send, tok_recv, w_sem, rim_send, rim_recv, st_send, st_recv,
+    middle, mid_send, mid_recv, solves, q_runs, k_tails, attends, fades,
 ):
     seq, me = lax.axis_index("seq"), lax.axis_index("tp")
     rows = hidden.shape[0]
     total = tokens.shape[0]
-    heads = rate_ref.shape[0]
+    heads = rate_ref.shape[1]
     head_dim = gain_ref.shape[1]
     taps = conv_ref.shape[1]
     last_tp, last_seq = n_tp - 1, n_seq - 1
-
-    own = pltpu.make_async_copy(hidden, tokens.at[pl.ds(me * rows, rows)], tok_recv.at[0])
+    square = n_tp == 4 and rows == CHUNK
+    part = rows // 2
+
+    own = pltpu.make_async_copy(hidden, tokens.at[pl.ds(me * rows, rows)], tok_recv.at[0, 0])
     own.start()
     loads = [pltpu.make_async_copy(w_qkv.at[b], weights.at[b], w_sem.at[b]) for b in range(3)]
     loads.append(pltpu.make_async_copy(w_gate, weights.at[3], w_sem.at[3]))
-    for load in loads:
+    small = [(rate_hbm, rate_ref), (bias_hbm, bias_ref), (wdb_hbm, wdb_ref), (conv_hbm, conv_ref), (gain_hbm, gain_ref)]
+    smalls = [pltpu.make_async_copy(src, dst, small_sem.at[i]) for i, (src, dst) in enumerate(small)]
+    for load in loads + smalls:
         load.start()
 
     barrier = pltpu.get_barrier_semaphore()
@@ -88,13 +94,43 @@
     pl.semaphore_wait(barrier, last_tp + before + after + after * tail_owner * last_tp)
 
     def token_copy(step):
-        peer = peer_of(me, step, n_tp)
         return pltpu.make_async_remote_copy(
             src_ref=hidden,
             dst_ref=tokens.at[pl.ds(me * rows, rows)],
-            send_sem=tok_send.at[step],
-            recv_sem=tok_recv.at[step],
-            device_id={"tp": peer},
+            send_sem=tok_send.at[step, 0],
+            recv_sem=tok_recv.at[step, 0],
+            device_id={"tp": peer_of(me, step, n_tp)},
+            device_id_type=MESH,
+        )
+
+    def part_copy(step, half):
+        return pltpu.make_async_remote_copy(
+            src_ref=hidden.at[pl.ds(half * part, part)],
+            dst_ref=tokens.at[pl.ds(me * rows + half * part, part)],
+            send_sem=tok_send.at[step, half],
+            recv_sem=tok_recv.at[step, half],
+            device_id={"tp": peer_of(me, step, n_tp)},
+            device_id_type=MESH,
+        )
+
+    def relay_copy(half):
+        there = tokens.at[pl.ds(peer_of(me, 2 - half, n_tp) * rows + half * part, part)]
+        return pltpu.make_async_remote_copy(
+            src_ref=there,
+            dst_ref=there,
+            send_sem=tok_send.at[3, half],
+            recv_sem=tok_recv.at[3, half],
+            device_id={"tp": peer_of(me, 1 + half, n_tp)},
+            device_id_type=MESH,
+        )
+
+    def middle_copy(target):
+        return pltpu.make_async_remote_copy(
+            src_ref=hidden.at[pl.ds(rows - RIM, RIM)],
+            dst_ref=middle,
+            send_sem=mid_send.at[target - 2],
+            recv_sem=mid_recv,
+            device_id={"tp": target},
             device_id_type=MESH,
         )
 
@@ -108,20 +144,30 @@
             device_id_type=MESH,
         )
 
-    for step in range(1, n_tp):
-        token_copy(step).start()
-
     @pl.when(jnp.logical_and(seq < last_seq, me == last_tp))
     def _():
         for target in range(n_tp):
             rim_copy(target).start()
 
+    if square:
+
+        @pl.when(me == 1)
+        def _():
+            for target in (2, 3):
+                middle_copy(target).start()
+
+        for step, half in ((1, 1), (2, 0), (1, 0), (2, 1)):
+            part_copy(step, half).start()
+    else:
+        for step in range(1, n_tp):
+            token_copy(step).start()
+
     @pl.when(seq == 0)
     def _():
         rim[...] = jnp.zeros_like(rim)
         st_in[...] = jnp.zeros_like(st_in)
 
-    for load in loads:
+    for load in loads + smalls:
         load.wait()
 
     def project(block, at):
@@ -133,23 +179,16 @@
 
         lax.fori_loop(0, 4, one, 0)
 
-    for step in range(n_tp):
-        if step == 0:
-            own.wait()
-        else:
-            token_copy(step).wait_recv()
-        if n_tp & (n_tp - 1):
-            slot = lax.rem(me - step + n_tp, n_tp)
-        else:
-            slot = peer_of(me, step, n_tp)
+    def project_slot(slot):
         at = pl.multiple_of(slot * rows, 16)
         project(tokens[pl.ds(at, rows), :], RIM + at)
 
-    @pl.when(seq > 0)
-    def _():
-        pltpu.make_async_copy(hidden.at[pl.ds(0, RIM)], rim, rim_recv).wait()
-
-    project(rim[...], 0)
+    def project_rim():
+        @pl.when(seq > 0)
+        def _():
+            pltpu.make_async_copy(hidden.at[pl.ds(0, RIM)], rim, rim_recv).wait()
+
+        project(rim[...], 0)
 
     down = lax.broadcasted_iota(jnp.int32, (CHUNK, CHUNK), 0)
     across = lax.broadcasted_iota(jnp.int32, (CHUNK, CHUNK), 1)
@@ -159,10 +198,12 @@
     for h in range(heads):
         state[h] = start
 
-    def chunk(c, carry):
+    wdb = low(jnp.concatenate([wdb_ref[0].astype(jnp.float32), wdb_ref[1].astype(jnp.float32)], axis=0))
+
+    def prepare(c):
         r0 = pl.multiple_of(c * CHUNK, CHUNK)
         scalars = lax.dot_general(
-            wdb_ref[...], tokens[pl.ds(r0, CHUNK), :], NT, preferred_element_type=jnp.float32
+            wdb, tokens[pl.ds(r0, CHUNK), :], NT, preferred_element_type=jnp.float32
         )
         per_head = []
         for h in range(heads):
@@ -179,8 +220,8 @@
             q = unit_rows(branch[0]) * (1.0 / math.sqrt(head_dim))
             k = unit_rows(branch[1])
             v = branch[2]
-            u = scalars[h : h + 1, :] + bias_ref[h]
-            log_row = -rate_ref[h] * (jnp.maximum(u, 0.0) + jnp.log1p(jnp.exp(-jnp.abs(u))))
+            u = scalars[h : h + 1, :] + bias_ref[0:1, h : h + 1]
+            log_row = -rate_ref[0:1, h : h + 1] * (jnp.maximum(u, 0.0) + jnp.log1p(jnp.exp(-jnp.abs(u))))
             rate_row = 1.0 / (1.0 + jnp.exp(-scalars[heads + h : heads + h + 1, :]))
             cum_col = jnp.sum(jnp.where(across <= down, log_row, 0.0), axis=1, keepdims=True)
             cum_row = jnp.sum(jnp.where(across == down, cum_col, 0.0), axis=0, keepdims=True)
@@ -192,33 +233,80 @@
             attend = weight * dot(q, k, NT)
             run = jnp.exp(cum_col)
             tail = rate_col * jnp.exp(end - cum_col)
-            per_head.append((q * run, k * run, v, k * tail, mixing, attend, jnp.exp(end)))
-        inverse = [eye] * heads
+            q_runs[c, h] = low(q * run)
+            k_tails[c, h] = low(k * tail)
+            attends[c, h] = low(attend)
+            fades[c, h] = jnp.broadcast_to(jnp.exp(end), (1, head_dim))
+            per_head.append((mixing, low(jnp.concatenate([v, k * run], axis=1))))
+        return per_head
+
+    def local(chunks):
+        chains = [(c, h) + item for c in chunks for h, item in enumerate(prepare(c))]
+        inverse = [None] * len(chains)
         size = 1
         while size < CHUNK:
             half = (down // size) % 2 == 1
             lower = jnp.logical_and(half, across // size == down // size - 1)
-            for h in range(heads):
-                part = jnp.where(lower, per_head[h][4], 0.0)
+            for i, (_, _, mixing, _) in enumerate(chains):
+                corner = jnp.where(lower, mixing, 0.0)
                 if size == 1:
-                    inverse[h] = eye - part
+                    inverse[i] = eye - corner
                 else:
-                    inverse[h] = inverse[h] - dot(dot(inverse[h], part), inverse[h])
+                    inverse[i] = inverse[i] - dot(dot(inverse[i], corner), inverse[i])
             size *= 2
+        for i, (c, h, _, right) in enumerate(chains):
+            solves[c, h] = dot(inverse[i], right)
+
+    def advance(c, carry):
+        r0 = pl.multiple_of(c * CHUNK, CHUNK)
         for h in range(heads):
-            q_run, k_run, v, k_tail, _, attend, fade = per_head[h]
-            solved = dot(inverse[h], jnp.concatenate([v, k_run], axis=1))
+            solved = solves[c, h]
             held = state[h]
             fresh = solved[:, :head_dim]
             fresh = jnp.concatenate([fresh, jnp.zeros_like(fresh)], axis=1)
             fresh = fresh - dot(solved[:, head_dim:], held)
-            read = dot(q_run, held) + dot(attend, fresh)
-            state[h] = fade * held + dot(k_tail, fresh, TN)
+            read = dot(q_runs[c, h], held) + dot(attends[c, h], fresh)
+            fade = jnp.concatenate([fades[c, h]] * 2, axis=1)
+            state[h] = fade * held + dot(k_tails[c, h], fresh, TN)
             outs[h, pl.ds(r0, CHUNK), :] = read[:, :head_dim]
             deltas[h, pl.ds(r0, CHUNK), :] = low(read[:, head_dim:])
         return carry
 
-    lax.fori_loop(0, total // CHUNK, chunk, 0)
+    count = total // CHUNK
+    own.wait()
+    project_slot(me)
+    if square:
+        part_copy(1, 1).wait_recv()
+        relay_copy(1).start()
+        part_copy(2, 0).wait_recv()
+        relay_copy(0).start()
+        project_rim()
+
+        @pl.when(me >= 2)
+        def _():
+            pltpu.make_async_copy(hidden.at[pl.ds(0, RIM)], middle, mid_recv).wait()
+            project(middle[...], 2 * rows)
+
+        part_copy(1, 0).wait_recv()
+        project_slot(peer_of(me, 1, n_tp))
+        first = 2 * (me // 2)
+        local((first, first + 1))
+        part_copy(2, 1).wait_recv()
+        project_slot(peer_of(me, 2, n_tp))
+        relay_copy(0).wait_recv()
+        relay_copy(1).wait_recv()
+        project_slot(peer_of(me, 3, n_tp))
+        local((2 - first, 3 - first))
+    else:
+        for step in range(1, n_tp):
+            token_copy(step).wait_recv()
+            if n_tp & (n_tp - 1):
+                project_slot(lax.rem(me - step + n_tp, n_tp))
+            else:
+                project_slot(peer_of(me, step, n_tp))
+        project_rim()
+        lax.fori_loop(0, count, lambda c, carry: (local((c,)), carry)[1], 0)
+    lax.fori_loop(0, count, advance, 0)
 
     def state_copy(h):
         return pltpu.make_async_remote_copy(
@@ -249,8 +337,19 @@
         gate = silu(proj[3, pl.ds(RIM, total), cols])
         out_ref[:, cols] = low(read * scale * gain_ref[...] * gate)
 
-    for step in range(1, n_tp):
-        token_copy(step).wait_send()
+    if square:
+        for half in range(2):
+            part_copy(1, half).wait_send()
+            part_copy(2, half).wait_send()
+            relay_copy(half).wait_send()
+
+        @pl.when(me == 1)
+        def _():
+            for target in (2, 3):
+                middle_copy(target).wait_send()
+    else:
+        for step in range(1, n_tp):
+            token_copy(step).wait_send()
 
     @pl.when(jnp.logical_and(seq < last_seq, me == last_tp))
     def _():
@@ -272,19 +371,21 @@
     columns = heads * head_dim
     rows = hidden.shape[0]
     total = rows * n_tp
-    wdb = w_decay_beta.transpose(1, 2, 0).reshape(2 * heads, width)
-    vmem, smem, anywhere = (
-        pl.BlockSpec(memory_space=pltpu.VMEM),
-        pl.BlockSpec(memory_space=pltpu.SMEM),
-        pl.BlockSpec(memory_space=pl.ANY),
-    )
+    vmem, anywhere = pl.BlockSpec(memory_space=pltpu.VMEM), pl.BlockSpec(memory_space=pl.ANY)
     dma = pltpu.SemaphoreType.DMA
+    count = total // CHUNK
     return pl.pallas_call(
         functools.partial(kernel, n_seq, n_tp),
         out_shape=jax.ShapeDtypeStruct((total, columns), jnp.bfloat16),
-        in_specs=[smem, smem, anywhere, anywhere, anywhere, vmem, vmem, vmem],
+        in_specs=[anywhere] * 8,
         out_specs=vmem,
         scratch_shapes=[
+            pltpu.VMEM((1, heads), jnp.float32),
+            pltpu.VMEM((1, heads), jnp.float32),
+            pltpu.VMEM((2, heads, width), jnp.bfloat16),
+            pltpu.VMEM((3, conv_weight.shape[0], columns), jnp.bfloat16),
+            pltpu.VMEM((1, head_dim), jnp.float32),
+            dma((5,)),
             pltpu.VMEM((total, width), jnp.bfloat16),
             pltpu.VMEM((RIM, width), jnp.bfloat16),
             pltpu.VMEM((4, width, columns), jnp.bfloat16),
@@ -294,19 +395,28 @@
             pltpu.VMEM((heads, total, head_dim), jnp.bfloat16),
             pltpu.VMEM((heads, head_dim, head_dim), jnp.bfloat16),
             pltpu.VMEM((heads, head_dim, head_dim), jnp.bfloat16),
-            dma((n_tp,)),
-            dma((n_tp,)),
+            dma((n_tp, 2)),
+            dma((n_tp, 2)),
             dma((4,)),
             dma((n_tp,)),
             dma,
             dma((heads,)),
             dma((heads,)),
+            pltpu.VMEM((RIM, width), jnp.bfloat16),
+            dma((2,)),
+            dma,
+            pltpu.VMEM((count, heads, CHUNK, 2 * head_dim), jnp.float32),
+            pltpu.VMEM((count, heads, CHUNK, head_dim), jnp.bfloat16),
+            pltpu.VMEM((count, heads, CHUNK, head_dim), jnp.bfloat16),
+            pltpu.VMEM((count, heads, CHUNK, CHUNK), jnp.bfloat16),
+            pltpu.VMEM((count, heads, 1, head_dim), jnp.float32),
         ],
         compiler_params=pltpu.CompilerParams(
-            collective_id=0, has_side_effects=True, vmem_limit_bytes=50 * 1024 * 1024
+            collective_id=0, has_side_effects=True, vmem_limit_bytes=60 * 1024 * 1024
         ),
     )(
-        decay_rate, dt_bias, hidden, w_qkv.transpose(1, 0, 2), w_gate, wdb,
+        decay_rate.reshape(1, heads), dt_bias.reshape(1, heads), hidden,
+        w_qkv.transpose(1, 0, 2), w_gate, w_decay_beta.transpose(1, 2, 0),
         conv_weight.transpose(1, 0, 2), norm_gain.reshape(1, head_dim),
     )
 

time: 65.5 us -> 50.1 us (0.76)
  Pallas kernels: 58.2 us -> 48.1 us
  local copies, waits for them, and re-layouts: 6.86 us -> 1.87 us
    pallas_call x1, Pallas kernels: 58.2 us -> 48.1 us  [per_device(): pl.pallas_call(functools.partial(kernel, n_seq, n_tp), out_shape=jax.Shap...]
    unnamed x13 -> x1, local copies, waits for them, and re-layouts: 6.09 us -> 1.87 us
    reshape x1 -> x0, local copies, waits for them, and re-layouts: 0.77 us -> none  [per_device(): wdb = w_decay_beta.transpose(1, 2, 0).reshape(2 * heads, width)]
where the time goes in v1:
time: 50.1 us; the launch traced here: 50 us
  Pallas kernels  48.1 us (96%)
  local copies, waits for them, and re-layouts  1.87 us (4%)
    pallas_call x1, Pallas kernels, per_device(): pl.pallas_call(functools.partial(kernel, n_seq, n_tp), out_shape=jax.Shap...  48.1 us
    unnamed x1, local copies, waits for them, and re-layouts  1.87 us

profile of v1, /device:TPU:25, one launch (start us, length us, event | category | flops | bytes accessed | tf_op | source)
XLA Modules:
  0.0 50.0 jit_solution(11021012708647620134)
XLA Ops:
  0.0 48.1 %shard_map.82 = bf16[512,512]{1,0:T(8,128)(2,1)} custom-call(f32[1,4]{1,0:T(1,128)} %bitcast.9, f32[1,4]{1,0:T(1,128)} %bitcast.10, bf16[128,2048]{1,0:T(8,128)(2,1)} %hidden.1, bf16[3,2048,512]{2,1,0:T(8,128)(2,1)} %bitcast.6, bf16[2048,512]{1,0:T(8,128)(2,1)} %w_gate.1, bf16[2,4,2048]{2,1,0:T(4,128)(2,1)} %bitcast.7, bf16[3,4,512]{2,1,0:T(4,128)(2,1)} %bitcast.8, ...), custom_call_target="tpu_custom_call" | custom-call | tf_op jit(solution)/shard_map/pallas_call | solution.py:377
  48.1 1.9 %copy.10 = bf16[512,512]{1,0:T(8,128)(2,1)} copy(bf16[512,512]{1,0:T(8,128)(2,1)} %shard_map.82) | data formatting | bytes 1048576
